TPU v7x, 256 devices: a whole 4x4x8 slice. The times are simulated.
256 devices in a mesh: rep: 64 (over z, x, core), rows: 4 (over y).
Axes of the slice: x: 4, y: 4, z: 8, core: 2. Of those that a mesh axis runs over, the one named last changes fastest.
Arguments:
- pooled_grad: bfloat16 [262144, 2, 128], P(('rep', 'rows')), may hold values from -6 to 6
- slot_source: int32 [256, 4, 1024], P(('rep', 'rows')), may hold values from 0 to 2047, as said below
- slot_target: int32 [256, 4, 1024], P(('rep', 'rows')), may hold values from 0 to 8191, as said below
- slot_count: int32 [256, 4], P(('rep', 'rows')), may hold values from 128 to 1024, as said below
- table_rows: float32 [2, 16384, 128], P(None, 'rows'), may hold values from -1.5 to 1.5
- accum: float32 [2, 16384], P(None, 'rows'), may hold values from 0.01 to 1
Outputs:
- new_rows: float32 [2, 16384, 128], P(None, 'rows')
- new_accum: float32 [2, 16384], P(None, 'rows')
Inputs may be any that keep to these rules, and one draw needn't show every extreme that they name: `slot_source`: entry q encodes a local sample q // 2 and a table q % 2; the table agrees with that of slot_target at the same slot. `slot_target`: entry t encodes a table t // 4096 and a row t % 4096 of the owner's shard; rows repeat across slots and senders. `slot_count`: slots at or past the count carry no lookup; every sender fills all slots to some owner.
All inputs are finite; a program needn't handle non-finite values.
Results may differ from a plain program's by a relative error of at most 0.0003.
Values may be sent and summed in bfloat16 or wider, within the bound.
No kernel may reach another device: no remote copies, remote signals or barrier semaphores. Data moves between devices by JAX's collectives and lax.ppermute only.
A program may use at most 64 MiB of HBM per device.

v0:
```python
import math
import jax
import jax.numpy as jnp
from jax import lax
from jax.sharding import Mesh
from jax.sharding import PartitionSpec as P

REP_ROWS = ("rep_0", "rep_1", "rep_2", "rows")
LEARN_RATE = 0.1
EPSILON = 1e-06


def rows_for(lines, count):
    spare = -len(lines) % count
    return jnp.pad(lines, [(0, spare)] + [(0, 0)] * (lines.ndim - 1))


def copy_for_each(shard, axis):
    count = lax.axis_size(axis)
    return lax.all_to_all(
        jnp.broadcast_to(shard[None], (count, *shard.shape)), axis, 0, 0, tiled=True
    )


def in_order(parts, dim):
    shape = list(parts.shape[1:])
    shape[dim] *= parts.shape[0]
    return jnp.moveaxis(parts, 0, dim).reshape(shape)


def gather_axes(shard, axes, dim):
    far, near = axes
    leading = copy_for_each(shard, far)
    parts = jnp.swapaxes(copy_for_each(leading, near), 0, 1)
    return in_order(parts.reshape(-1, *shard.shape), dim)


def in_blocks(shard, dim, count):
    shape = shard.shape
    parts = shard.reshape(*shape[:dim], count, shape[dim] // count, *shape[dim + 1 :])
    return jnp.moveaxis(parts, dim, 0)


def summed_on_arrival(shard, axis, dim):
    count = lax.axis_size(axis)
    parts = lax.all_to_all(in_blocks(shard, dim, count), axis, 0, 0, tiled=True)
    return jnp.sum(parts, axis=0)


def sum_by_axis(shard, axes, dim):
    far, near = axes
    own = summed_on_arrival(in_blocks(shard, dim, lax.axis_size(far)), near, dim + 1)
    return jnp.sum(lax.all_to_all(own, far, 0, 0, tiled=True), axis=0)


def nested_sum(shard, axes):
    lines = shard.reshape(-1, shard.shape[-1])
    padded = rows_for(lines, lax.axis_size(axes[0]) * lax.axis_size(axes[1]))
    whole = gather_axes(sum_by_axis(padded, axes, 0), axes, 0)
    return lax.slice_in_dim(whole, 0, len(lines)).reshape(shard.shape)


def accumulate(grads, targets, tables, rows_dev):
    feature = grads.shape[-1]
    flat_rows = grads.reshape(-1, feature)
    lookup_keys = targets.reshape(-1)
    row_total = tables * rows_dev
    block_size = math.gcd(row_total, 512)
    block_count = row_total // block_size
    offsets = jnp.arange(block_size, dtype=jnp.int32)

    def row_block(block_index):
        row_base = block_index * block_size
        matches = (lookup_keys[:, None] == row_base + offsets[None, :]).astype(jnp.bfloat16)
        return jnp.einsum("sr,sw->rw", matches, flat_rows, preferred_element_type=jnp.float32)

    blocks = lax.map(row_block, jnp.arange(block_count, dtype=jnp.int32))
    return blocks.reshape(tables, rows_dev, feature)


def pick_rows(flat_grad, lookup_keys):
    slot_total = lookup_keys.shape[0]
    block_size = math.gcd(slot_total, 1024)
    block_count = slot_total // block_size
    sources = jnp.arange(flat_grad.shape[0], dtype=jnp.int32)
    key_blocks = lookup_keys.reshape(block_count, block_size)

    def slot_block(block_keys):
        matches = (block_keys[:, None] == sources[None, :]).astype(jnp.bfloat16)
        return jnp.dot(matches, flat_grad, preferred_element_type=jnp.float32).astype(jnp.bfloat16)

    blocks = lax.map(slot_block, key_blocks)
    return blocks.reshape(slot_total, flat_grad.shape[1])


def adagrad(rows_part, state_part, row_grad):
    updated = state_part + jnp.mean(row_grad * row_grad, axis=2)
    shifted = rows_part - LEARN_RATE * row_grad / (jnp.sqrt(updated)[:, :, None] + EPSILON)
    return (shifted, updated)


def shards(pooled_grad, slot_source, slot_target, slot_count, table_rows, accum):
    tables = pooled_grad.shape[1]
    feature = pooled_grad.shape[2]
    rows_dev = table_rows.shape[1]
    owner_total = slot_source.shape[1]
    slot_total = slot_source.shape[2]
    flat_grad = pooled_grad.reshape(-1, feature)
    source = slot_source[0]
    target = slot_target[0]
    counts = slot_count[0]
    slot_ids = jnp.arange(slot_total, dtype=jnp.int32)
    filled = slot_ids[None, :] < counts[:, None]
    source_keys = jnp.where(filled, source, -1).reshape(-1)
    picked = pick_rows(flat_grad, source_keys).reshape(owner_total, slot_total, feature)
    targets = jnp.where(filled, target, -1)
    got_grads, got_targets = (
        lax.all_to_all(picked, "rows", split_axis=0, concat_axis=0, tiled=True),
        lax.all_to_all(targets, "rows", split_axis=0, concat_axis=0, tiled=True),
    )
    partial_grad = accumulate(got_grads, got_targets, tables, rows_dev)
    row_grad = nested_sum(partial_grad, (("rep_0", "rep_1"), "rep_2"))
    new_rows, new_accum = adagrad(table_rows, accum, row_grad)
    return (new_rows, new_accum)


def solution(mesh):
    split = Mesh(
        mesh.devices.reshape(8, 4, 2, mesh.shape["rows"]), ("rep_0", "rep_1", "rep_2", "rows")
    )
    placed = (
        P(REP_ROWS, None, None),
        P(REP_ROWS, None, None),
        P(REP_ROWS, None, None),
        P(REP_ROWS, None),
        P(None, "rows", None),
        P(None, "rows"),
    )
    return jax.shard_map(
        shards,
        mesh=split,
        in_specs=placed,
        out_specs=(P(None, "rows", None), P(None, "rows")),
        check_vma=False,
    )
```

profile of v0, /device:TPU:1, one launch (start us, length us, event | category | flops | bytes accessed | tf_op | source)
XLA Modules:
  0.0 269.6 jit_solution(3844847864048092937)
XLA Ops:
  2.0 5.0 %all-to-all-start = ((s32[4,1,1024]{2,1,0:T(1,128)}), s32[4,1,1024]{2,1,0:T(1,128)S(1)}, u32[]{:S(2)}, u32[]{:S(2)}) async-start(s32[4,1,1024]{2,1,0:T(1,128)} %compare_select_fusion), calls=%async_computation | async-start | bytes 32768 | tf_op jit(solution)/shard_map/all_to_all | solution.py:119
  7.8 12.9 %while.22 = (s32[]{:T(128)}, bf16[4,1024,128]{2,1,0:T(8,128)(2,1)}, s32[4,1024]{1,0:T(4,128)S(1)}, bf16[2048,128]{1,0:T(8,128)(2,1)}, s32[]{:T(128)}) while((s32[]{:T(128)}, bf16[4,1024,128]{2,1,0:T(8,128)(2,1)}, s32[4,1024]{1,0:T(4,128)S(1)}, bf16[2048,128]{1,0:T(8,128)(2,1)}, s32[]{:T(128)}) %tuple.50), condition=%wide.region_1.2_spmd.clone, body=%wide.region_0.1_spmd.clone.sunk | while | flops 539099136 | bytes 799297 | solution.py:92
  20.7 4.2 %all-to-all-start.1 = ((bf16[4,1024,128]{2,1,0:T(8,128)(2,1)}), bf16[4,1024,128]{2,1,0:T(8,128)(2,1)S(1)}, u32[]{:S(2)}, u32[]{:S(2)}) async-start(bf16[4,1024,128]{2,1,0:T(8,128)(2,1)} %get-tuple-element.61), calls=%async_computation.1 | async-start | bytes 2097152 | tf_op jit(solution)/shard_map/all_to_all | solution.py:118
  25.0 13.2 %all-to-all-done.1 = bf16[4,1024,128]{2,1,0:T(8,128)(2,1)S(1)} async-done(((bf16[4,1024,128]{2,1,0:T(8,128)(2,1)}), bf16[4,1024,128]{2,1,0:T(8,128)(2,1)S(1)}, u32[]{:S(2)}, u32[]{:S(2)}) %all-to-all-start.1) | async-done | bytes 1048608 | tf_op jit(solution)/shard_map/all_to_all | solution.py:118
  38.2 78.5 %while.23 = (s32[]{:T(128)}, f32[16,512,128]{2,1,0:T(8,128)}, s32[4,1024]{1,0:T(4,128)S(1)}, s32[16]{0:T(128)S(1)}, bf16[4096,128]{1,0:T(8,128)(2,1)S(1)}, /*index=5*/s32[]{:T(128)}, s32[1]{0:T(128)}) while((s32[]{:T(128)}, f32[16,512,128]{2,1,0:T(8,128)}, s32[4,1024]{1,0:T(4,128)S(1)}, s32[16]{0:T(128)S(1)}, ...), condition=%wide.region_3.4_spmd.clone, body=%wide.region_2.3_spmd.clone.sunk | while | flops 538968576 | bytes 1364585 | solution.py:77
  39.4 3.7 %fusion.30 = f32[16,512,128]{2,1,0:T(8,128)} fusion(f32[16,512,128]{2,1,0:T(8,128)} %get-tuple-element.184, s32[]{:T(128)} %get-tuple-element.183, bf16[4096,128]{1,0:T(8,128)(2,1)S(1)} %get-tuple-element.194, s32[512]{0:T(512)S(1)} %iota_add_fusion.2, s32[4096]{0:T(1024)S(1)} %bitcast.53), kind=kOutput, calls=%fused_computation.14.clone.1 | convolution fusion | flops 538968064 | bytes 1329664 | tf_op jit(solution)/shard_map/while/body/eval_jaxpr/sr,sw->rw/dot_general | solution.py:75
  44.3 3.7 %fusion.30 = f32[16,512,128]{2,1,0:T(8,128)} fusion(f32[16,512,128]{2,1,0:T(8,128)} %get-tuple-element.184, s32[]{:T(128)} %get-tuple-element.183, bf16[4096,128]{1,0:T(8,128)(2,1)S(1)} %get-tuple-element.194, s32[512]{0:T(512)S(1)} %iota_add_fusion.2, s32[4096]{0:T(1024)S(1)} %bitcast.53), kind=kOutput, calls=%fused_computation.14.clone.1 | convolution fusion | flops 538968064 | bytes 1329664 | tf_op jit(solution)/shard_map/while/body/eval_jaxpr/sr,sw->rw/dot_general | solution.py:75
  49.3 3.7 %fusion.30 = f32[16,512,128]{2,1,0:T(8,128)} fusion(f32[16,512,128]{2,1,0:T(8,128)} %get-tuple-element.184, s32[]{:T(128)} %get-tuple-element.183, bf16[4096,128]{1,0:T(8,128)(2,1)S(1)} %get-tuple-element.194, s32[512]{0:T(512)S(1)} %iota_add_fusion.2, s32[4096]{0:T(1024)S(1)} %bitcast.53), kind=kOutput, calls=%fused_computation.14.clone.1 | convolution fusion | flops 538968064 | bytes 1329664 | tf_op jit(solution)/shard_map/while/body/eval_jaxpr/sr,sw->rw/dot_general | solution.py:75
  54.2 3.7 %fusion.30 = f32[16,512,128]{2,1,0:T(8,128)} fusion(f32[16,512,128]{2,1,0:T(8,128)} %get-tuple-element.184, s32[]{:T(128)} %get-tuple-element.183, bf16[4096,128]{1,0:T(8,128)(2,1)S(1)} %get-tuple-element.194, s32[512]{0:T(512)S(1)} %iota_add_fusion.2, s32[4096]{0:T(1024)S(1)} %bitcast.53), kind=kOutput, calls=%fused_computation.14.clone.1 | convolution fusion | flops 538968064 | bytes 1329664 | tf_op jit(solution)/shard_map/while/body/eval_jaxpr/sr,sw->rw/dot_general | solution.py:75
  59.1 3.7 %fusion.30 = f32[16,512,128]{2,1,0:T(8,128)} fusion(f32[16,512,128]{2,1,0:T(8,128)} %get-tuple-element.184, s32[]{:T(128)} %get-tuple-element.183, bf16[4096,128]{1,0:T(8,128)(2,1)S(1)} %get-tuple-element.194, s32[512]{0:T(512)S(1)} %iota_add_fusion.2, s32[4096]{0:T(1024)S(1)} %bitcast.53), kind=kOutput, calls=%fused_computation.14.clone.1 | convolution fusion | flops 538968064 | bytes 1329664 | tf_op jit(solution)/shard_map/while/body/eval_jaxpr/sr,sw->rw/dot_general | solution.py:75
  64.0 3.7 %fusion.30 = f32[16,512,128]{2,1,0:T(8,128)} fusion(f32[16,512,128]{2,1,0:T(8,128)} %get-tuple-element.184, s32[]{:T(128)} %get-tuple-element.183, bf16[4096,128]{1,0:T(8,128)(2,1)S(1)} %get-tuple-element.194, s32[512]{0:T(512)S(1)} %iota_add_fusion.2, s32[4096]{0:T(1024)S(1)} %bitcast.53), kind=kOutput, calls=%fused_computation.14.clone.1 | convolution fusion | flops 538968064 | bytes 1329664 | tf_op jit(solution)/shard_map/while/body/eval_jaxpr/sr,sw->rw/dot_general | solution.py:75
  68.9 3.7 %fusion.30 = f32[16,512,128]{2,1,0:T(8,128)} fusion(f32[16,512,128]{2,1,0:T(8,128)} %get-tuple-element.184, s32[]{:T(128)} %get-tuple-element.183, bf16[4096,128]{1,0:T(8,128)(2,1)S(1)} %get-tuple-element.194, s32[512]{0:T(512)S(1)} %iota_add_fusion.2, s32[4096]{0:T(1024)S(1)} %bitcast.53), kind=kOutput, calls=%fused_computation.14.clone.1 | convolution fusion | flops 538968064 | bytes 1329664 | tf_op jit(solution)/shard_map/while/body/eval_jaxpr/sr,sw->rw/dot_general | solution.py:75
  73.8 3.7 %fusion.30 = f32[16,512,128]{2,1,0:T(8,128)} fusion(f32[16,512,128]{2,1,0:T(8,128)} %get-tuple-element.184, s32[]{:T(128)} %get-tuple-element.183, bf16[4096,128]{1,0:T(8,128)(2,1)S(1)} %get-tuple-element.194, s32[512]{0:T(512)S(1)} %iota_add_fusion.2, s32[4096]{0:T(1024)S(1)} %bitcast.53), kind=kOutput, calls=%fused_computation.14.clone.1 | convolution fusion | flops 538968064 | bytes 1329664 | tf_op jit(solution)/shard_map/while/body/eval_jaxpr/sr,sw->rw/dot_general | solution.py:75
  78.7 3.7 %fusion.30 = f32[16,512,128]{2,1,0:T(8,128)} fusion(f32[16,512,128]{2,1,0:T(8,128)} %get-tuple-element.184, s32[]{:T(128)} %get-tuple-element.183, bf16[4096,128]{1,0:T(8,128)(2,1)S(1)} %get-tuple-element.194, s32[512]{0:T(512)S(1)} %iota_add_fusion.2, s32[4096]{0:T(1024)S(1)} %bitcast.53), kind=kOutput, calls=%fused_computation.14.clone.1 | convolution fusion | flops 538968064 | bytes 1329664 | tf_op jit(solution)/shard_map/while/body/eval_jaxpr/sr,sw->rw/dot_general | solution.py:75
  83.6 3.7 %fusion.30 = f32[16,512,128]{2,1,0:T(8,128)} fusion(f32[16,512,128]{2,1,0:T(8,128)} %get-tuple-element.184, s32[]{:T(128)} %get-tuple-element.183, bf16[4096,128]{1,0:T(8,128)(2,1)S(1)} %get-tuple-element.194, s32[512]{0:T(512)S(1)} %iota_add_fusion.2, s32[4096]{0:T(1024)S(1)} %bitcast.53), kind=kOutput, calls=%fused_computation.14.clone.1 | convolution fusion | flops 538968064 | bytes 1329664 | tf_op jit(solution)/shard_map/while/body/eval_jaxpr/sr,sw->rw/dot_general | solution.py:75
  88.5 3.7 %fusion.30 = f32[16,512,128]{2,1,0:T(8,128)} fusion(f32[16,512,128]{2,1,0:T(8,128)} %get-tuple-element.184, s32[]{:T(128)} %get-tuple-element.183, bf16[4096,128]{1,0:T(8,128)(2,1)S(1)} %get-tuple-element.194, s32[512]{0:T(512)S(1)} %iota_add_fusion.2, s32[4096]{0:T(1024)S(1)} %bitcast.53), kind=kOutput, calls=%fused_computation.14.clone.1 | convolution fusion | flops 538968064 | bytes 1329664 | tf_op jit(solution)/shard_map/while/body/eval_jaxpr/sr,sw->rw/dot_general | solution.py:75
  93.4 3.7 %fusion.30 = f32[16,512,128]{2,1,0:T(8,128)} fusion(f32[16,512,128]{2,1,0:T(8,128)} %get-tuple-element.184, s32[]{:T(128)} %get-tuple-element.183, bf16[4096,128]{1,0:T(8,128)(2,1)S(1)} %get-tuple-element.194, s32[512]{0:T(512)S(1)} %iota_add_fusion.2, s32[4096]{0:T(1024)S(1)} %bitcast.53), kind=kOutput, calls=%fused_computation.14.clone.1 | convolution fusion | flops 538968064 | bytes 1329664 | tf_op jit(solution)/shard_map/while/body/eval_jaxpr/sr,sw->rw/dot_general | solution.py:75
  98.3 3.7 %fusion.30 = f32[16,512,128]{2,1,0:T(8,128)} fusion(f32[16,512,128]{2,1,0:T(8,128)} %get-tuple-element.184, s32[]{:T(128)} %get-tuple-element.183, bf16[4096,128]{1,0:T(8,128)(2,1)S(1)} %get-tuple-element.194, s32[512]{0:T(512)S(1)} %iota_add_fusion.2, s32[4096]{0:T(1024)S(1)} %bitcast.53), kind=kOutput, calls=%fused_computation.14.clone.1 | convolution fusion | flops 538968064 | bytes 1329664 | tf_op jit(solution)/shard_map/while/body/eval_jaxpr/sr,sw->rw/dot_general | solution.py:75
  103.2 3.7 %fusion.30 = f32[16,512,128]{2,1,0:T(8,128)} fusion(f32[16,512,128]{2,1,0:T(8,128)} %get-tuple-element.184, s32[]{:T(128)} %get-tuple-element.183, bf16[4096,128]{1,0:T(8,128)(2,1)S(1)} %get-tuple-element.194, s32[512]{0:T(512)S(1)} %iota_add_fusion.2, s32[4096]{0:T(1024)S(1)} %bitcast.53), kind=kOutput, calls=%fused_computation.14.clone.1 | convolution fusion | flops 538968064 | bytes 1329664 | tf_op jit(solution)/shard_map/while/body/eval_jaxpr/sr,sw->rw/dot_general | solution.py:75
  108.2 3.7 %fusion.30 = f32[16,512,128]{2,1,0:T(8,128)} fusion(f32[16,512,128]{2,1,0:T(8,128)} %get-tuple-element.184, s32[]{:T(128)} %get-tuple-element.183, bf16[4096,128]{1,0:T(8,128)(2,1)S(1)} %get-tuple-element.194, s32[512]{0:T(512)S(1)} %iota_add_fusion.2, s32[4096]{0:T(1024)S(1)} %bitcast.53), kind=kOutput, calls=%fused_computation.14.clone.1 | convolution fusion | flops 538968064 | bytes 1329664 | tf_op jit(solution)/shard_map/while/body/eval_jaxpr/sr,sw->rw/dot_general | solution.py:75
  119.2 10.6 %all_to_all.34 = f32[2,32,128,128]{3,2,1,0:T(8,128)} all-to-all(f32[2,32,128,128]{3,2,1,0:T(8,128)S(1)} %copy.15), channel_id=1, replica_groups=mesh['rep_0'=8,'rep_1'=4,'rep_2'=2,'rows'=4] {'rep_2'}, dimensions={0} | all-to-all | bytes 8388608 | tf_op jit(solution)/shard_map/all_to_all | solution.py:46
  132.5 59.8 %all_to_all.35 = f32[32,128,128]{2,1,0:T(8,128)} all-to-all(f32[32,128,128]{2,1,0:T(8,128)S(1)} %reduce_sum.27), channel_id=1, replica_groups=mesh['rep_0'=8,'rep_1'=4,'rep_2'=2,'rows'=4] {'rep_0','rep_1'}, dimensions={0} | all-to-all | bytes 4194304 | tf_op jit(solution)/shard_map/all_to_all | solution.py:53
  194.2 54.1 %all_to_all.36 = f32[32,128,128]{2,1,0:T(8,128)S(1)} all-to-all(f32[32,128,128]{2,1,0:T(8,128)S(1)} %broadcast_in_dim.42), channel_id=1, replica_groups=mesh['rep_0'=8,'rep_1'=4,'rep_2'=2,'rows'=4] {'rep_0','rep_1'}, dimensions={0} | all-to-all | bytes 4194304 | tf_op jit(solution)/shard_map/all_to_all | solution.py:20
  248.9 10.2 %all_to_all.37 = f32[2,32,128,128]{3,2,1,0:T(8,128)S(1)} all-to-all(f32[2,32,128,128]{3,2,1,0:T(8,128)S(1)} %broadcast_in_dim.43), channel_id=1, replica_groups=mesh['rep_0'=8,'rep_1'=4,'rep_2'=2,'rows'=4] {'rep_2'}, dimensions={0} | all-to-all | bytes 8388608 | tf_op jit(solution)/shard_map/all_to_all | solution.py:20
  (82 shorter events, 46.2 us)
Async XLA Ops:
  2.0 18.7 %all-to-all-start = ((s32[4,1,1024]{2,1,0:T(1,128)}), s32[4,1,1024]{2,1,0:T(1,128)S(1)}, u32[]{:S(2)}, u32[]{:S(2)}) async-start(s32[4,1,1024]{2,1,0:T(1,128)} %compare_select_fusion), calls=%async_computation | async-start | bytes 32768 | tf_op jit(solution)/shard_map/all_to_all | solution.py:119
  20.7 17.4 %all-to-all-start.1 = ((bf16[4,1024,128]{2,1,0:T(8,128)(2,1)}), bf16[4,1024,128]{2,1,0:T(8,128)(2,1)S(1)}, u32[]{:S(2)}, u32[]{:S(2)}) async-start(bf16[4,1024,128]{2,1,0:T(8,128)(2,1)} %get-tuple-element.61), calls=%async_computation.1 | async-start | bytes 2097152 | tf_op jit(solution)/shard_map/all_to_all | solution.py:118
  259.0 2.0 copy-start
  261.1 1.3 copy-start.2
  263.0 3.4 %copy-start.1 = (f32[2,4096,128]{2,1,0:T(8,128)S(1)}, f32[2,4096,128]{2,1,0:T(8,128)}, u32[]{:S(2)}) copy-start(f32[2,4096,128]{2,1,0:T(8,128)} %param.14) | copy-start | bytes 12582916
where the time goes:
time: 270 us
  blocking collectives  135 us (50%)
  matrix products  71.3 us (26%)
  local copies, waits for them, and re-layouts  15.4 us (6%)
  other arithmetic  14.4 us (5%)
  waiting for transfers between devices  13.2 us (5%)
  loops' own time  10.7 us (4%)
  starting transfers between devices  9.24 us (3%)
    all_to_all x2, blocking collectives, copy_for_each(): lax.all_to_all(jnp.broadcast_to(shard[None], (count, *shard.shape)), axis...  64.3 us
    all_to_all x1, blocking collectives, sum_by_axis(): return jnp.sum(lax.all_to_all(own, far, 0, 0, tiled=True), axis=0)  59.8 us
    dot_general x16, matrix products, row_block(): jnp.einsum('sr,sw->rw', matches, flat_rows, preferred_element_type=jnp.fl...  58.4 us
    all_to_all x1, waiting for transfers between devices, shards(): lax.all_to_all(picked, 'rows', split_axis=0, concat_axis=0, tiled=True)  13.2 us
    dot_general x4, matrix products, slot_block(): jnp.dot(matches, flat_grad, preferred_element_type=jnp.float32)  12.9 us
    another operation x1, loops' own time, accumulate(): blocks = lax.map(row_block, jnp.arange(block_count, dtype=jnp.int32))  10.7 us
    all_to_all x1, blocking collectives, summed_on_arrival(): parts = lax.all_to_all(in_blocks(shard, dim, count), axis, 0, 0, tiled=True)  10.6 us
    dynamic_slice x16, local copies, waits for them, and re-layouts, accumulate(): blocks = lax.map(row_block, jnp.arange(block_count, dtype=jnp.int32))  9.32 us
  transfers between devices with their start and end apart: 2, of which 1 were waited for; matrix products, arithmetic and copies ran while one was open for 5% of the time, Pallas kernels for 0%

commit v1 on v0

--- a/solution.py
+++ b/solution.py
@@ -8,6 +8,32 @@
 REP_ROWS = ("rep_0", "rep_1", "rep_2", "rows")
 LEARN_RATE = 0.1
 EPSILON = 1e-06
+
+
+def load_zone(original, array_axis, work_x):
+    t1, y = (original.shape[:array_axis], original.shape[array_axis + 1 :])
+    return jnp.moveaxis(original.reshape(*t1, work_x, -1, *y), array_axis, 0)
+
+
+def shape_panel(t0, along_dim):
+    t0 = jnp.moveaxis(t0, 0, along_dim)
+    opened = t0.shape
+    return t0.reshape(
+        *opened[:along_dim], opened[along_dim] * opened[along_dim + 1], *opened[along_dim + 2 :]
+    )
+
+
+def connect_results_now(raw, along_axis, x_part, body):
+    out_arr, z2 = (lax.axis_size(along_axis), lax.axis_index(along_axis))
+    carry_in = load_zone(raw, x_part, out_arr)
+    column = [carry_in[z2]]
+    q = 1
+    while q < out_arr:
+        known = carry_in[z2 ^ q]
+        column.append(lax.ppermute(known, along_axis, [(rr, rr ^ q) for rr in range(out_arr)]))
+        q = q + 1
+    carry_in = jnp.stack(column)[z2 ^ jnp.arange(out_arr)]
+    return shape_panel(carry_in, body)
 
 
 def rows_for(lines, count):
@@ -115,7 +141,7 @@
     picked = pick_rows(flat_grad, source_keys).reshape(owner_total, slot_total, feature)
     targets = jnp.where(filled, target, -1)
     got_grads, got_targets = (
-        lax.all_to_all(picked, "rows", split_axis=0, concat_axis=0, tiled=True),
+        connect_results_now(picked, "rows", 0, body=0),
         lax.all_to_all(targets, "rows", split_axis=0, concat_axis=0, tiled=True),
     )
     partial_grad = accumulate(got_grads, got_targets, tables, rows_dev)

time: 270 us -> 263 us (0.974)
  waiting for transfers between devices: 13.2 us -> 8.98 us
    all_to_all x1 -> x0, waiting for transfers between devices: 13.2 us -> none  [shards(): lax.all_to_all(picked, 'rows', split_axis=0, concat_axis=0, tiled=True)]
    all_to_all x1, waiting for transfers between devices: 0.01 us -> 8.97 us  [shards(): lax.all_to_all(targets, 'rows', split_axis=0, concat_axis=0, tiled=True)]
    ppermute x0 -> x3, starting transfers between devices: none -> 4.82 us  [connect_results_now(): lax.ppermute(known, along_axis, [(rr, rr ^ q) for rr in range(out_arr)])]
    all_to_all x1 -> x0, starting transfers between devices: 4.24 us -> none  [shards(): lax.all_to_all(picked, 'rows', split_axis=0, concat_axis=0, tiled=True)]
  transfers between devices with their start and end apart: 2 -> 4, of which waited for: 1 -> 1; matrix products, arithmetic and copies ran while one was open for 5% -> 0% of each run, Pallas kernels for 0% -> 0%
where the time goes in v1:
time: 263 us; the launch traced here: 262 us
  blocking collectives  134 us (51%)
  matrix products  68.9 us (26%)
  local copies, waits for them, and re-layouts  16.2 us (6%)
  other arithmetic  13.8 us (5%)
  loops' own time  10.8 us (4%)
  waiting for transfers between devices  8.98 us (3%)
  starting transfers between devices  8.76 us (3%)
    all_to_all x2, blocking collectives, copy_for_each(): lax.all_to_all(jnp.broadcast_to(shard[None], (count, *shard.shape)), axis...  64.3 us
    all_to_all x1, blocking collectives, sum_by_axis(): return jnp.sum(lax.all_to_all(own, far, 0, 0, tiled=True), axis=0)  59.8 us
    dot_general x16, matrix products, row_block(): jnp.einsum('sr,sw->rw', matches, flat_rows, preferred_element_type=jnp.fl...  58.4 us
    another operation x1, loops' own time, accumulate(): blocks = lax.map(row_block, jnp.arange(block_count, dtype=jnp.int32))  10.7 us
    dot_general x4, matrix products, slot_block(): jnp.dot(matches, flat_grad, preferred_element_type=jnp.float32)  10.5 us
    all_to_all x1, blocking collectives, summed_on_arrival(): parts = lax.all_to_all(in_blocks(shard, dim, count), axis, 0, 0, tiled=True)  9.88 us
    dynamic_slice x16, local copies, waits for them, and re-layouts, accumulate(): blocks = lax.map(row_block, jnp.arange(block_count, dtype=jnp.int32))  9.32 us
    all_to_all x1, waiting for transfers between devices, shards(): lax.all_to_all(targets, 'rows', split_axis=0, concat_axis=0, tiled=True)  8.97 us
  transfers between devices with their start and end apart: 4, of which 1 were waited for; matrix products, arithmetic and copies ran while one was open for 0% of the time, Pallas kernels for 0%

profile of v1, /device:TPU:1, one launch (start us, length us, event | category | flops | bytes accessed | tf_op | source)
XLA Modules:
  0.0 262.2 jit_solution(12685457011015513224)
XLA Ops:
  1.5 10.6 %while.22 = (s32[]{:T(128)}, bf16[4,1024,128]{2,1,0:T(8,128)(2,1)S(1)}, s32[4,1024]{1,0:T(4,128)S(1)}, bf16[2048,128]{1,0:T(8,128)(2,1)}, s32[]{:T(128)}) while((s32[]{:T(128)}, bf16[4,1024,128]{2,1,0:T(8,128)(2,1)S(1)}, s32[4,1024]{1,0:T(4,128)S(1)}, bf16[2048,128]{1,0:T(8,128)(2,1)}, s32[]{:T(128)}) %tuple.53), condition=%wide.region_1.2_spmd.clone, body=%wide.region_0.1_spmd.clone.sunk | while | flops 539099136 | bytes 798789 | solution.py:118
  17.7 3.9 %all-to-all-start = ((s32[4,1,1024]{2,1,0:T(1,128)}), s32[4,1,1024]{2,1,0:T(1,128)S(1)}, u32[]{:S(2)}, u32[]{:S(2)}) async-start(s32[4,1,1024]{2,1,0:T(1,128)} %compare_select_fusion), calls=%async_computation | async-start | bytes 32768 | tf_op jit(solution)/shard_map/all_to_all | solution.py:145
  21.6 9.0 %all-to-all-done = s32[4,1,1024]{2,1,0:T(1,128)S(1)} async-done(((s32[4,1,1024]{2,1,0:T(1,128)}), s32[4,1,1024]{2,1,0:T(1,128)S(1)}, u32[]{:S(2)}, u32[]{:S(2)}) %all-to-all-start) | async-done | bytes 16416 | tf_op jit(solution)/shard_map/all_to_all | solution.py:145
  31.6 78.5 %while.23 = (s32[]{:T(128)}, f32[16,512,128]{2,1,0:T(8,128)}, s32[4,1024]{1,0:T(4,128)S(1)}, s32[16]{0:T(128)S(1)}, bf16[4096,128]{1,0:T(8,128)(2,1)S(1)}, /*index=5*/s32[]{:T(128)}, s32[1]{0:T(128)}) while((s32[]{:T(128)}, f32[16,512,128]{2,1,0:T(8,128)}, s32[4,1024]{1,0:T(4,128)S(1)}, s32[16]{0:T(128)S(1)}, ...), condition=%wide.region_3.4_spmd.clone, body=%wide.region_2.3_spmd.clone.sunk | while | flops 538968576 | bytes 1364585 | solution.py:103
  32.8 3.7 %fusion.31 = f32[16,512,128]{2,1,0:T(8,128)} fusion(f32[16,512,128]{2,1,0:T(8,128)} %get-tuple-element.188, s32[]{:T(128)} %get-tuple-element.187, bf16[4096,128]{1,0:T(8,128)(2,1)S(1)} %get-tuple-element.198, s32[512]{0:T(512)S(1)} %iota_add_fusion.2, s32[4096]{0:T(1024)S(1)} %bitcast.62), kind=kOutput, calls=%fused_computation.15.clone.1 | convolution fusion | flops 538968064 | bytes 1329664 | tf_op jit(solution)/shard_map/while/body/eval_jaxpr/sr,sw->rw/dot_general | solution.py:101
  37.7 3.7 %fusion.31 = f32[16,512,128]{2,1,0:T(8,128)} fusion(f32[16,512,128]{2,1,0:T(8,128)} %get-tuple-element.188, s32[]{:T(128)} %get-tuple-element.187, bf16[4096,128]{1,0:T(8,128)(2,1)S(1)} %get-tuple-element.198, s32[512]{0:T(512)S(1)} %iota_add_fusion.2, s32[4096]{0:T(1024)S(1)} %bitcast.62), kind=kOutput, calls=%fused_computation.15.clone.1 | convolution fusion | flops 538968064 | bytes 1329664 | tf_op jit(solution)/shard_map/while/body/eval_jaxpr/sr,sw->rw/dot_general | solution.py:101
  42.6 3.7 %fusion.31 = f32[16,512,128]{2,1,0:T(8,128)} fusion(f32[16,512,128]{2,1,0:T(8,128)} %get-tuple-element.188, s32[]{:T(128)} %get-tuple-element.187, bf16[4096,128]{1,0:T(8,128)(2,1)S(1)} %get-tuple-element.198, s32[512]{0:T(512)S(1)} %iota_add_fusion.2, s32[4096]{0:T(1024)S(1)} %bitcast.62), kind=kOutput, calls=%fused_computation.15.clone.1 | convolution fusion | flops 538968064 | bytes 1329664 | tf_op jit(solution)/shard_map/while/body/eval_jaxpr/sr,sw->rw/dot_general | solution.py:101
  47.6 3.7 %fusion.31 = f32[16,512,128]{2,1,0:T(8,128)} fusion(f32[16,512,128]{2,1,0:T(8,128)} %get-tuple-element.188, s32[]{:T(128)} %get-tuple-element.187, bf16[4096,128]{1,0:T(8,128)(2,1)S(1)} %get-tuple-element.198, s32[512]{0:T(512)S(1)} %iota_add_fusion.2, s32[4096]{0:T(1024)S(1)} %bitcast.62), kind=kOutput, calls=%fused_computation.15.clone.1 | convolution fusion | flops 538968064 | bytes 1329664 | tf_op jit(solution)/shard_map/while/body/eval_jaxpr/sr,sw->rw/dot_general | solution.py:101
  52.5 3.7 %fusion.31 = f32[16,512,128]{2,1,0:T(8,128)} fusion(f32[16,512,128]{2,1,0:T(8,128)} %get-tuple-element.188, s32[]{:T(128)} %get-tuple-element.187, bf16[4096,128]{1,0:T(8,128)(2,1)S(1)} %get-tuple-element.198, s32[512]{0:T(512)S(1)} %iota_add_fusion.2, s32[4096]{0:T(1024)S(1)} %bitcast.62), kind=kOutput, calls=%fused_computation.15.clone.1 | convolution fusion | flops 538968064 | bytes 1329664 | tf_op jit(solution)/shard_map/while/body/eval_jaxpr/sr,sw->rw/dot_general | solution.py:101
  57.4 3.7 %fusion.31 = f32[16,512,128]{2,1,0:T(8,128)} fusion(f32[16,512,128]{2,1,0:T(8,128)} %get-tuple-element.188, s32[]{:T(128)} %get-tuple-element.187, bf16[4096,128]{1,0:T(8,128)(2,1)S(1)} %get-tuple-element.198, s32[512]{0:T(512)S(1)} %iota_add_fusion.2, s32[4096]{0:T(1024)S(1)} %bitcast.62), kind=kOutput, calls=%fused_computation.15.clone.1 | convolution fusion | flops 538968064 | bytes 1329664 | tf_op jit(solution)/shard_map/while/body/eval_jaxpr/sr,sw->rw/dot_general | solution.py:101
  62.3 3.7 %fusion.31 = f32[16,512,128]{2,1,0:T(8,128)} fusion(f32[16,512,128]{2,1,0:T(8,128)} %get-tuple-element.188, s32[]{:T(128)} %get-tuple-element.187, bf16[4096,128]{1,0:T(8,128)(2,1)S(1)} %get-tuple-element.198, s32[512]{0:T(512)S(1)} %iota_add_fusion.2, s32[4096]{0:T(1024)S(1)} %bitcast.62), kind=kOutput, calls=%fused_computation.15.clone.1 | convolution fusion | flops 538968064 | bytes 1329664 | tf_op jit(solution)/shard_map/while/body/eval_jaxpr/sr,sw->rw/dot_general | solution.py:101
  67.2 3.7 %fusion.31 = f32[16,512,128]{2,1,0:T(8,128)} fusion(f32[16,512,128]{2,1,0:T(8,128)} %get-tuple-element.188, s32[]{:T(128)} %get-tuple-element.187, bf16[4096,128]{1,0:T(8,128)(2,1)S(1)} %get-tuple-element.198, s32[512]{0:T(512)S(1)} %iota_add_fusion.2, s32[4096]{0:T(1024)S(1)} %bitcast.62), kind=kOutput, calls=%fused_computation.15.clone.1 | convolution fusion | flops 538968064 | bytes 1329664 | tf_op jit(solution)/shard_map/while/body/eval_jaxpr/sr,sw->rw/dot_general | solution.py:101
  72.1 3.7 %fusion.31 = f32[16,512,128]{2,1,0:T(8,128)} fusion(f32[16,512,128]{2,1,0:T(8,128)} %get-tuple-element.188, s32[]{:T(128)} %get-tuple-element.187, bf16[4096,128]{1,0:T(8,128)(2,1)S(1)} %get-tuple-element.198, s32[512]{0:T(512)S(1)} %iota_add_fusion.2, s32[4096]{0:T(1024)S(1)} %bitcast.62), kind=kOutput, calls=%fused_computation.15.clone.1 | convolution fusion | flops 538968064 | bytes 1329664 | tf_op jit(solution)/shard_map/while/body/eval_jaxpr/sr,sw->rw/dot_general | solution.py:101
  77.0 3.7 %fusion.31 = f32[16,512,128]{2,1,0:T(8,128)} fusion(f32[16,512,128]{2,1,0:T(8,128)} %get-tuple-element.188, s32[]{:T(128)} %get-tuple-element.187, bf16[4096,128]{1,0:T(8,128)(2,1)S(1)} %get-tuple-element.198, s32[512]{0:T(512)S(1)} %iota_add_fusion.2, s32[4096]{0:T(1024)S(1)} %bitcast.62), kind=kOutput, calls=%fused_computation.15.clone.1 | convolution fusion | flops 538968064 | bytes 1329664 | tf_op jit(solution)/shard_map/while/body/eval_jaxpr/sr,sw->rw/dot_general | solution.py:101
  81.9 3.7 %fusion.31 = f32[16,512,128]{2,1,0:T(8,128)} fusion(f32[16,512,128]{2,1,0:T(8,128)} %get-tuple-element.188, s32[]{:T(128)} %get-tuple-element.187, bf16[4096,128]{1,0:T(8,128)(2,1)S(1)} %get-tuple-element.198, s32[512]{0:T(512)S(1)} %iota_add_fusion.2, s32[4096]{0:T(1024)S(1)} %bitcast.62), kind=kOutput, calls=%fused_computation.15.clone.1 | convolution fusion | flops 538968064 | bytes 1329664 | tf_op jit(solution)/shard_map/while/body/eval_jaxpr/sr,sw->rw/dot_general | solution.py:101
  86.8 3.7 %fusion.31 = f32[16,512,128]{2,1,0:T(8,128)} fusion(f32[16,512,128]{2,1,0:T(8,128)} %get-tuple-element.188, s32[]{:T(128)} %get-tuple-element.187, bf16[4096,128]{1,0:T(8,128)(2,1)S(1)} %get-tuple-element.198, s32[512]{0:T(512)S(1)} %iota_add_fusion.2, s32[4096]{0:T(1024)S(1)} %bitcast.62), kind=kOutput, calls=%fused_computation.15.clone.1 | convolution fusion | flops 538968064 | bytes 1329664 | tf_op jit(solution)/shard_map/while/body/eval_jaxpr/sr,sw->rw/dot_general | solution.py:101
  91.7 3.7 %fusion.31 = f32[16,512,128]{2,1,0:T(8,128)} fusion(f32[16,512,128]{2,1,0:T(8,128)} %get-tuple-element.188, s32[]{:T(128)} %get-tuple-element.187, bf16[4096,128]{1,0:T(8,128)(2,1)S(1)} %get-tuple-element.198, s32[512]{0:T(512)S(1)} %iota_add_fusion.2, s32[4096]{0:T(1024)S(1)} %bitcast.62), kind=kOutput, calls=%fused_computation.15.clone.1 | convolution fusion | flops 538968064 | bytes 1329664 | tf_op jit(solution)/shard_map/while/body/eval_jaxpr/sr,sw->rw/dot_general | solution.py:101
  96.6 3.7 %fusion.31 = f32[16,512,128]{2,1,0:T(8,128)} fusion(f32[16,512,128]{2,1,0:T(8,128)} %get-tuple-element.188, s32[]{:T(128)} %get-tuple-element.187, bf16[4096,128]{1,0:T(8,128)(2,1)S(1)} %get-tuple-element.198, s32[512]{0:T(512)S(1)} %iota_add_fusion.2, s32[4096]{0:T(1024)S(1)} %bitcast.62), kind=kOutput, calls=%fused_computation.15.clone.1 | convolution fusion | flops 538968064 | bytes 1329664 | tf_op jit(solution)/shard_map/while/body/eval_jaxpr/sr,sw->rw/dot_general | solution.py:101
  101.5 3.7 %fusion.31 = f32[16,512,128]{2,1,0:T(8,128)} fusion(f32[16,512,128]{2,1,0:T(8,128)} %get-tuple-element.188, s32[]{:T(128)} %get-tuple-element.187, bf16[4096,128]{1,0:T(8,128)(2,1)S(1)} %get-tuple-element.198, s32[512]{0:T(512)S(1)} %iota_add_fusion.2, s32[4096]{0:T(1024)S(1)} %bitcast.62), kind=kOutput, calls=%fused_computation.15.clone.1 | convolution fusion | flops 538968064 | bytes 1329664 | tf_op jit(solution)/shard_map/while/body/eval_jaxpr/sr,sw->rw/dot_general | solution.py:101
  106.5 3.7 %fusion.31 = f32[16,512,128]{2,1,0:T(8,128)} fusion(f32[16,512,128]{2,1,0:T(8,128)} %get-tuple-element.188, s32[]{:T(128)} %get-tuple-element.187, bf16[4096,128]{1,0:T(8,128)(2,1)S(1)} %get-tuple-element.198, s32[512]{0:T(512)S(1)} %iota_add_fusion.2, s32[4096]{0:T(1024)S(1)} %bitcast.62), kind=kOutput, calls=%fused_computation.15.clone.1 | convolution fusion | flops 538968064 | bytes 1329664 | tf_op jit(solution)/shard_map/while/body/eval_jaxpr/sr,sw->rw/dot_general | solution.py:101
  112.6 9.9 %all_to_all.29 = f32[2,32,128,128]{3,2,1,0:T(8,128)} all-to-all(f32[2,32,128,128]{3,2,1,0:T(8,128)S(1)} %copy.15), channel_id=1, replica_groups=mesh['rep_0'=8,'rep_1'=4,'rep_2'=2,'rows'=4] {'rep_2'}, dimensions={0} | all-to-all | bytes 8388608 | tf_op jit(solution)/shard_map/all_to_all | solution.py:72
  125.2 59.8 %all_to_all.30 = f32[32,128,128]{2,1,0:T(8,128)} all-to-all(f32[32,128,128]{2,1,0:T(8,128)S(1)} %reduce_sum.27), channel_id=1, replica_groups=mesh['rep_0'=8,'rep_1'=4,'rep_2'=2,'rows'=4] {'rep_0','rep_1'}, dimensions={0} | all-to-all | bytes 4194304 | tf_op jit(solution)/shard_map/all_to_all | solution.py:79
  186.9 54.1 %all_to_all.31 = f32[32,128,128]{2,1,0:T(8,128)S(1)} all-to-all(f32[32,128,128]{2,1,0:T(8,128)S(1)} %broadcast_in_dim.43), channel_id=1, replica_groups=mesh['rep_0'=8,'rep_1'=4,'rep_2'=2,'rows'=4] {'rep_0','rep_1'}, dimensions={0} | all-to-all | bytes 4194304 | tf_op jit(solution)/shard_map/all_to_all | solution.py:46
  241.5 10.2 %all_to_all.32 = f32[2,32,128,128]{3,2,1,0:T(8,128)S(1)} all-to-all(f32[2,32,128,128]{3,2,1,0:T(8,128)S(1)} %broadcast_in_dim.44), channel_id=1, replica_groups=mesh['rep_0'=8,'rep_1'=4,'rep_2'=2,'rows'=4] {'rep_2'}, dimensions={0} | all-to-all | bytes 8388608 | tf_op jit(solution)/shard_map/all_to_all | solution.py:46
  (95 shorter events, 45.3 us)
Async XLA Ops:
  1.4 15.5 %copy-start.3 = (s32[1,4,1024]{2,1,0:T(4,128)S(1)}, s32[1,4,1024]{2,1,0:T(4,128)}, u32[]{:S(2)}) copy-start(s32[1,4,1024]{2,1,0:T(4,128)} %param.12) | copy-start | bytes 49156
  1.4 15.5 %copy-start.4 = (s32[1,4]{1,0:T(1,128)S(1)}, s32[1,4]{1,0:T(1,128)}, u32[]{:S(2)}) copy-start(s32[1,4]{1,0:T(1,128)} %param.13) | copy-start | bytes 52
  12.2 18.5 %collective-permute-start = (bf16[1,1024,128]{2,1,0:T(8,128)(2,1)S(1)}, bf16[1,1024,128]{2,1,0:T(8,128)(2,1)S(1)}, u32[]{:S(2)}, u32[]{:S(2)}) collective-permute-start(bf16[1,1024,128]{2,1,0:T(8,128)(2,1)S(1)} %get-tuple-element.107), channel_id=1, source_target_pairs={{0,1},{1,0},{2,3},{3,2},{4,5},{5,4},{6,7},{7,6},{8,9},{9,8},{10,11... | collective-permute-start | bytes 786440 | tf_op jit(solution)/shard_map/ppermute | solution.py:33
  14.4 16.3 %collective-permute-start.1 = (bf16[1,1024,128]{2,1,0:T(8,128)(2,1)S(1)}, bf16[1,1024,128]{2,1,0:T(8,128)(2,1)S(1)}, u32[]{:S(2)}, u32[]{:S(2)}) collective-permute-start(bf16[1,1024,128]{2,1,0:T(8,128)(2,1)S(1)} %get-tuple-element.106), channel_id=1, source_target_pairs={{0,2},{1,3},{2,0},{3,1},{4,6},{5,7},{6,4},{7,5},{8,10},{9,11},{10,... | collective-permute-start | bytes 786440 | tf_op jit(solution)/shard_map/ppermute | solution.py:33
  17.0 13.7 %collective-permute-start.2 = (bf16[1,1024,128]{2,1,0:T(8,128)(2,1)S(1)}, bf16[1,1024,128]{2,1,0:T(8,128)(2,1)S(1)}, u32[]{:S(2)}, u32[]{:S(2)}) collective-permute-start(bf16[1,1024,128]{2,1,0:T(8,128)(2,1)S(1)} %get-tuple-element.108), channel_id=1, source_target_pairs={{0,3},{1,2},{2,1},{3,0},{4,7},{5,6},{6,5},{7,4},{8,11},{9,10},{10,... | collective-permute-start | bytes 786440 | tf_op jit(solution)/shard_map/ppermute | solution.py:33
  17.7 12.9 %all-to-all-start = ((s32[4,1,1024]{2,1,0:T(1,128)}), s32[4,1,1024]{2,1,0:T(1,128)S(1)}, u32[]{:S(2)}, u32[]{:S(2)}) async-start(s32[4,1,1024]{2,1,0:T(1,128)} %compare_select_fusion), calls=%async_computation | async-start | bytes 32768 | tf_op jit(solution)/shard_map/all_to_all | solution.py:145
  251.7 2.0 copy-start
  253.7 1.3 copy-start.2
  255.6 3.4 %copy-start.1 = (f32[2,4096,128]{2,1,0:T(8,128)S(1)}, f32[2,4096,128]{2,1,0:T(8,128)}, u32[]{:S(2)}) copy-start(f32[2,4096,128]{2,1,0:T(8,128)} %param.14) | copy-start | bytes 12582916
